TPU v7x, 256 devices: a whole 4x4x8 slice. The times are simulated.
256 devices in a mesh: task: 4 (over z_lo), tile: 64 (over y, z_hi, x, core).
Axes of the slice: x: 4, y: 4, z: 8 (z_hi: 2, z_lo: 4; z = z_hi * 4 + z_lo), core: 2. Of those that a mesh axis runs over, the one named last changes fastest.
Arguments:
- adjusted: bfloat16 [8, 3584, 18944], P('task', 'tile'), may hold values from -6 to 6
- fisher: bfloat16 [8, 3584, 18944], P('task', 'tile'), may hold values from 0.0099487305 to 10
Outputs:
- merged: bfloat16 [3584, 18944], P(None, ('task', 'tile'))
All inputs are finite; a program needn't handle non-finite values.
Results may differ from a plain program's by a relative error of at most 0.001.
Values may be sent and summed in bfloat16 or wider, within the bound.
A program may use at most 64 MiB of HBM per device.

v0:
```python
import jax
import jax.numpy as jnp
from jax import lax
from jax.sharding import PartitionSpec as P


def in_one_piece(arrays, axis, dim, along):
    both = jnp.concatenate(arrays, axis=along)
    out, at, outs = (lax.psum_scatter(both, axis, scatter_dimension=dim, tiled=True), 0, [])
    for a in arrays:
        outs.append(lax.slice_in_dim(out, at, at + a.shape[along], axis=along))
        at += a.shape[along]
    return tuple(outs)


def body(adjusted, fisher):
    scaled = fisher.astype(jnp.float32)
    numerator = jnp.sum(scaled * adjusted.astype(jnp.float32), axis=0)
    denominator = jnp.sum(scaled, axis=0)
    summed_num, summed_den = in_one_piece((numerator, denominator), "task", 1, 0)
    owner_num, owner_den = (
        lax.all_to_all(summed_num, "tile", split_axis=1, concat_axis=0, tiled=True),
        lax.all_to_all(summed_den, "tile", split_axis=1, concat_axis=0, tiled=True),
    )
    merged = (owner_num / owner_den).astype(jnp.bfloat16)
    return merged


def solution(mesh):
    return jax.shard_map(
        body,
        mesh=mesh,
        in_specs=(P("task", "tile", None), P("task", "tile", None)),
        out_specs=P(None, ("task", "tile")),
        check_vma=False,
    )
```

profile of v0, /device:TPU:1, one launch (start us, length us, event | category | flops | bytes accessed | tf_op | source)
XLA Modules:
  0.0 299.3 jit_solution(2950465631684679464)
XLA Ops:
  6.5 0.0 reduce-scatter.2.cloned.1.call-start
  6.5 6.1 %fusion = (f32[56,18944]{1,0:T(8,128)S(1)}, f32[56,18944]{1,0:T(8,128)S(1)}) fusion(bf16[2,56,18944]{2,1,0:T(8,128)(2,1)} %param.3, bf16[2,56,18944]{2,1,0:T(8,128)(2,1)} %param.2), kind=kLoop, calls=%fused_computation.2 | loop fusion | flops 8486912 | bytes 16973824 | tf_op jit(solution)/shard_map/reduce_sum | solution.py:18
  12.6 3.8 %pad_maximum_fusion = f32[112,18944]{1,0:T(8,128)} fusion(f32[56,18944]{1,0:T(8,128)S(1)} %get-tuple-element.6, f32[56,18944]{1,0:T(8,128)S(1)} %get-tuple-element.5), kind=kLoop, calls=%fused_computation.3 | loop fusion | flops 2121728 | bytes 16973824 | tf_op jit(solution)/shard_map/concatenate | solution.py:8
  16.4 0.0 reduce-scatter.2.cloned.1.call-update
  16.5 155.3 %reduce-scatter.2.cloned.1.call-done = f32[112,4736]{1,0:T(8,128)} async-done(((f32[112,18944]{1,0:T(8,128)}), f32[112,4736]{1,0:T(8,128)}) %reduce-scatter.2.cloned.1.call-update) | async-done | bytes 2121744 | tf_op jit(solution)/shard_map/reduce_scatter | solution.py:9
  171.8 2.7 fusion.1
  174.5 4.0 %all_to_all.22 = f32[56,64,74]{2,1,0:T(8,128)S(1)} reshape(f32[56,4736]{1,0:T(8,128)} %get-tuple-element.7) | data formatting | bytes 2121728 | tf_op jit(solution)/shard_map/all_to_all | solution.py:23
  178.5 2.3 copy.6
  180.8 12.1 %all-to-all-start.1 = ((f32[56,64,74]{2,0,1:T(8,128)}), f32[56,64,74]{2,0,1:T(8,128)S(1)}, u32[]{:S(2)}, u32[]{:S(2)}) async-start(f32[56,64,74]{2,0,1:T(8,128)} %copy.6), calls=%async_computation.2 | async-start | bytes 3670016 | tf_op jit(solution)/shard_map/all_to_all | solution.py:23
  192.9 4.1 %all_to_all.20 = f32[56,64,74]{2,1,0:T(8,128)} reshape(f32[56,4736]{1,0:T(8,128)S(1)} %get-tuple-element.8) | data formatting | bytes 2121728 | tf_op jit(solution)/shard_map/all_to_all | solution.py:22
  197.0 3.8 %copy.5 = f32[56,64,74]{2,0,1:T(8,128)} copy(f32[56,64,74]{2,1,0:T(8,128)} %all_to_all.20) | data formatting | bytes 2121728 | tf_op jit(solution)/shard_map/all_to_all | solution.py:22
  200.8 26.1 %all-to-all-done.1 = f32[56,64,74]{2,0,1:T(8,128)S(1)} async-done(((f32[56,64,74]{2,0,1:T(8,128)}), f32[56,64,74]{2,0,1:T(8,128)S(1)}, u32[]{:S(2)}, u32[]{:S(2)}) %all-to-all-start.1) | async-done | bytes 1060896 | tf_op jit(solution)/shard_map/all_to_all | solution.py:23
  226.9 63.9 %all_to_all.26 = f32[56,64,74]{2,0,1:T(8,128)S(1)} all-to-all(f32[56,64,74]{2,0,1:T(8,128)} %copy.5), channel_id=1, replica_groups=mesh['task'=4,'tile'=64] {'tile'}, dimensions={1} | all-to-all | bytes 2121728 | tf_op jit(solution)/shard_map/all_to_all | solution.py:22
  290.8 0.4 divide_convert_fusion
  291.2 1.2 copy.7
Async XLA Ops:
  6.5 165.3 %reduce-scatter.2.cloned.1.call-start = ((), (), s32[]{:S(2)}) async-start(), calls=%async_computation.3 | async-start | bytes 10608640 | tf_op jit(solution)/shard_map/reduce_scatter | solution.py:9
  180.8 46.1 %all-to-all-start.1 = ((f32[56,64,74]{2,0,1:T(8,128)}), f32[56,64,74]{2,0,1:T(8,128)S(1)}, u32[]{:S(2)}, u32[]{:S(2)}) async-start(f32[56,64,74]{2,0,1:T(8,128)} %copy.6), calls=%async_computation.2 | async-start | bytes 3670016 | tf_op jit(solution)/shard_map/all_to_all | solution.py:23
Sparse Core Ops, SparseCore 0:
  16.6 155.1 reduce-scatter.1
where the time goes:
time: 302 us; the launch traced here: 299 us
  waiting for transfers between devices  181 us (60%)
  blocking collectives  63.9 us (21%)
  local copies, waits for them, and re-layouts  18.1 us (6%)
  between operations  13.4 us (4%)
  starting transfers between devices  12.1 us (4%)
  other arithmetic  10.3 us (3%)
    reduce_scatter x1, waiting for transfers between devices, in_one_piece(): lax.psum_scatter(both, axis, scatter_dimension=dim, tiled=True)  155 us
    all_to_all x1, blocking collectives, body(): lax.all_to_all(summed_num, 'tile', split_axis=1, concat_axis=0, tiled=True)  63.9 us
    all_to_all x1, waiting for transfers between devices, body(): lax.all_to_all(summed_den, 'tile', split_axis=1, concat_axis=0, tiled=True)  26.1 us
    all_to_all x1, starting transfers between devices, body(): lax.all_to_all(summed_den, 'tile', split_axis=1, concat_axis=0, tiled=True)  12.1 us
    all_to_all x2, local copies, waits for them, and re-layouts, body(): lax.all_to_all(summed_num, 'tile', split_axis=1, concat_axis=0, tiled=True)  7.92 us
    all_to_all x2, local copies, waits for them, and re-layouts, body(): lax.all_to_all(summed_den, 'tile', split_axis=1, concat_axis=0, tiled=True)  6.32 us
    reduce_sum x1, other arithmetic, body(): numerator = jnp.sum(scaled * adjusted.astype(jnp.float32), axis=0)  6.06 us
  transfers between devices with their start and end apart: 2, of which 2 were waited for; matrix products, arithmetic and copies ran while one was open for 1% of the time, Pallas kernels for 0%

commit v1 on v0

v1 whole, which is shorter than its diff:
```python
import functools
import math

import jax
import jax.numpy as jnp
from jax import lax
from jax.experimental import pallas as pl
from jax.experimental.pallas import tpu as pltpu
from jax.sharding import PartitionSpec as P

MESH = pl.DeviceIdType.MESH
F32 = jnp.float32
BF16 = jnp.bfloat16

ROWS, TILES, LANES = 7, 37, 128
QUARTER = TILES * LANES
SEG, SEG_PAD, OWN = 592, 640, 74
PIECES = ((0, 19), (19, 18))
GROUP = 5
STEPS = 2 * ROWS
AHEAD, LAG, SKEW = 5, 3, 2

Q_POWER, Q_TOP, Q_KNEE = 24.0, 120.0, -9.5
Q_FLOOR = 2.0 ** (Q_TOP + Q_POWER * Q_KNEE)
Q_LINE = Q_FLOOR / 2.0**Q_KNEE
D_POWER, D_MID = 25.0, -1.665
INV_LN2 = 1.0 / math.log(2.0)


def log2(x):
    return jnp.log(x) * INV_LN2


def encode_q(q, inverse_scale):
    y = jnp.abs(q) * inverse_scale
    knee = 2.0**Q_KNEE
    power = jnp.exp2(log2(jnp.maximum(y, knee)) * Q_POWER + Q_TOP)
    code = jnp.where(y >= knee, power, y * Q_LINE)
    return jnp.where(q < 0, -code, code).astype(BF16)


def decode_q(code, scale):
    c = code.astype(F32)
    size = jnp.abs(c)
    root = jnp.exp2((log2(jnp.maximum(size, Q_FLOOR)) - Q_TOP) * (1.0 / Q_POWER))
    y = jnp.where(size >= Q_FLOOR, root, size * (1.0 / Q_LINE)) * scale
    return jnp.where(c < 0, -y, y)


def encode_d(d, log_count):
    return jnp.exp2((log2(d) - (log_count + D_MID)) * D_POWER).astype(BF16)


def decode_d(code, log_count):
    return jnp.exp2(log2(code.astype(F32)) * (1.0 / D_POWER) + (log_count + D_MID))


def lanes(tile, count=1):
    start = tile * LANES
    return pl.ds(start if isinstance(start, int) else pl.multiple_of(start, LANES), count * LANES)


def groups(start, count):
    return [range(a, min(a + GROUP, start + count)) for a in range(start, start + count, GROUP)]


def kernel(a_hbm, f_hbm, out, av, fv, up_in, up_out, dn_in, dn_out, merged, seg_out, seg_in, split,
           in_sem, chain_recv, chain_send, seg_recv, seg_send, out_recv, out_send):
    task, tile = lax.axis_index("task"), lax.axis_index("tile")
    slot, side = tile // 8, tile % 8

    def loads(r):
        return (pltpu.make_async_copy(a_hbm.at[:, r], av.at[:, r], in_sem.at[0, r]),
                pltpu.make_async_copy(f_hbm.at[:, r], fv.at[:, r], in_sem.at[1, r]))

    for r in range(ROWS):
        for copy in loads(r):
            copy.start()

    barrier = pltpu.get_barrier_semaphore()
    place = task * 8 + slot

    def greet_column(i, carry):
        other = (place + i) % 32
        pl.semaphore_signal(barrier, inc=1, device_id=(other // 8, (other % 8) * 8 + side), device_id_type=MESH)
        return carry

    def greet_side(i, carry):
        pl.semaphore_signal(barrier, inc=1, device_id=(task, slot * 8 + (side + i) % 8), device_id_type=MESH)
        return carry

    lax.fori_loop(1, 32, greet_column, 0)
    lax.fori_loop(1, 8, greet_side, 0)
    pl.semaphore_wait(barrier, 38)

    def wait_rows(i):
        @pl.when(i % 2 == 0)
        def _():
            for copy in loads(i // 2):
                copy.wait()

    def own(i, first_task, tiles):
        r, t = i // 2, i % 2
        base = (first_task + t) * TILES
        n, d = [], []
        for x in tiles:
            at = lanes(base + x)
            f0, f1 = fv[0, r, :, at].astype(F32), fv[1, r, :, at].astype(F32)
            n.append(f0 * av[0, r, :, at].astype(F32) + f1 * av[1, r, :, at].astype(F32))
            d.append(f0 + f1)
        return n, d

    def own_scale(i, first_task):
        r, t = i // 2, i % 2
        base = (first_task + t) * TILES
        tops = [jnp.full((8, LANES), 2.0**-96, F32) for _ in range(4)]
        for x in range(TILES):
            at = lanes(base + x)
            for m in range(2):
                k = (2 * x + m) % 4
                tops[k] = jnp.maximum(tops[k], jnp.abs(av[m, r, :, at].astype(F32)))
        return jnp.maximum(jnp.maximum(tops[0], tops[1]), jnp.maximum(tops[2], tops[3]))

    def span(piece):
        start, count = PIECES[piece]
        low = 0 if piece == 0 else 1 + 2 * start
        return pl.ds(low * LANES, (1 + 2 * (start + count) - low) * LANES)

    def hop(i, piece, source, target, way, to):
        r, t = i // 2, i % 2
        at = span(piece)
        return pltpu.make_async_remote_copy(
            src_ref=source.at[r, t, :, at], dst_ref=target.at[r, t, :, at],
            send_sem=chain_send.at[way], recv_sem=chain_recv.at[way, i, piece],
            device_id=(to, tile), device_id_type=MESH)

    def arrived(i, piece, target, way):
        r, t = i // 2, i % 2
        at = span(piece)
        pltpu.make_async_copy(target.at[r, t, :, at], target.at[r, t, :, at], chain_recv.at[way, i, piece]).wait()

    def received(i, piece, tiles, source, log_count, scale):
        r, t = i // 2, i % 2
        start, count = PIECES[piece]
        q = [decode_q(source[r, t, :, lanes(1 + start + x)], scale) for x in tiles]
        d = [decode_d(source[r, t, :, lanes(1 + start + count + x)], log_count) for x in tiles]
        return q, d

    def put(i, piece, tiles, n, d, target, log_count, inverse):
        r, t = i // 2, i % 2
        start, count = PIECES[piece]
        q = [encode_q(a / b, inverse) for a, b in zip(n, d)]
        e = [encode_d(b, log_count) for b in d]
        for x, code in zip(tiles, q):
            target[r, t, :, lanes(1 + start + x)] = code
        for x, code in zip(tiles, e):
            target[r, t, :, lanes(1 + start + count + x)] = code

    def first(i, first_task, way, target, landing, to):
        wait_rows(i)
        scale = own_scale(i, first_task)
        inverse = 1.0 / scale
        target[i // 2, i % 2, :, lanes(0)] = scale.astype(BF16)
        for piece, (start, count) in enumerate(PIECES):
            for tiles in groups(start, count):
                n, d = own(i, first_task, tiles)
                put(i, piece, tiles, n, d, target, 1.0, inverse)
            hop(i, piece, target, landing, way, to).start()

    def middle(i, first_task, way, source, target, to, log_in, log_out, wait_for_rows):
        if wait_for_rows:
            wait_rows(i)
        mine = own_scale(i, first_task)
        for piece, (start, count) in enumerate(PIECES):
            arrived(i, piece, source, way)
            if piece == 0:
                before = source[i // 2, i % 2, :, lanes(0)].astype(F32)
                scale = jnp.maximum(before, mine)
                inverse = 1.0 / scale
                target[i // 2, i % 2, :, lanes(0)] = scale.astype(BF16)
            for tiles in groups(start, count):
                n, d = own(i, first_task, tiles)
                q, e = received(i, piece, tiles, source, log_in, before)
                n = [x + a * b for x, a, b in zip(n, q, e)]
                d = [x + b for x, b in zip(d, e)]
                put(i, piece, tiles, n, d, target, log_out, inverse)
            hop(i, piece, target, source, way, to).start()

    lane = lax.broadcasted_iota(jnp.int32, (8, LANES), 1)

    def last(i, first_task, way, source):
        r, t = i // 2, i % 2
        for piece, (start, count) in enumerate(PIECES):
            arrived(i, piece, source, way)
            if piece == 0:
                before = source[r, t, :, lanes(0)].astype(F32)
            for tiles in groups(start, count):
                n, d = own(i, first_task, tiles)
                q, e = received(i, piece, tiles, source, math.log2(6.0), before)
                for x, n1, d1, q1, e1 in zip(tiles, n, d, q, e):
                    merged[:, lanes(x)] = (n1 + q1 * e1) / (d1 + e1)
        for k in range(8):
            low, off = SEG * k // LANES, SEG * k % LANES
            parts = [merged[:, lanes(low + j)] for j in range(6 if off else 5)]
            if off:
                parts = [pltpu.roll(x, LANES - off, 1) for x in parts]
                parts = [jnp.where(lane < LANES - off, parts[j], parts[j + 1]) for j in range(5)]
            for j in range(5):
                seg_out[r, t, k, :, lanes(j)] = parts[j].astype(BF16)
        for k in range(8):
            pltpu.make_async_remote_copy(
                src_ref=seg_out.at[r, t, k], dst_ref=seg_in.at[r, slot],
                send_sem=seg_send, recv_sem=seg_recv.at[r],
                device_id=(first_task + t, k * 8 + side), device_id_type=MESH).start()

    lane3 = lax.broadcasted_iota(jnp.int32, (8, 8, LANES), 2)

    def spread(r):
        pltpu.make_async_copy(seg_in.at[r], seg_in.at[r], seg_recv.at[r]).wait()
        for k in range(8):
            low, off = OWN * k // LANES, OWN * k % LANES
            part = seg_in[r, :, :, lanes(low)].astype(F32)
            if off:
                part = pltpu.roll(part, LANES - off, 2)
            if off + OWN > LANES:
                more = pltpu.roll(seg_in[r, :, :, lanes(low + 1)].astype(F32), LANES - off, 2)
                part = jnp.where(lane3 < LANES - off, part, more)
            split[r, k] = part.astype(BF16)
        pltpu.make_async_copy(split.at[r, side], out.at[:, side, r], out_recv).start()

        def send(i, carry):
            k = (side + i) % 8
            pltpu.make_async_remote_copy(
                src_ref=split.at[r, k], dst_ref=out.at[:, side, r],
                send_sem=out_send, recv_sem=out_recv,
                device_id=(task, slot * 8 + k), device_id_type=MESH).start()
            return carry

        lax.fori_loop(1, 8, send, 0)

    def loop(low, high, body):
        def step(i, carry):
            body(i)
            return carry

        lax.fori_loop(low, high, step, 0)

    def outer(send_task, send_way, target, landing, to, merge_task, merge_way, source):
        def go(i):
            first(i, send_task, send_way, target, landing, to)

        loop(0, AHEAD, go)

        def step(i):
            last(i, merge_task, merge_way, source)

            @pl.when(i + AHEAD < STEPS)
            def _():
                go(i + AHEAD)

            @pl.when((i % 2 == 1) & (i // 2 >= LAG))
            def _():
                spread(i // 2 - LAG)

        loop(0, STEPS, step)
        loop(ROWS - LAG, ROWS, spread)

    def inner(lead, trail):
        def step(i):
            @pl.when(i < STEPS)
            def _():
                lead(i, True)

            @pl.when(i >= SKEW)
            def _():
                trail(i - SKEW, False)

            @pl.when((i % 2 == 1) & (i // 2 >= LAG))
            def _():
                spread(i // 2 - LAG)

        loop(0, STEPS + SKEW, step)
        loop((STEPS + SKEW) // 2 - LAG, ROWS, spread)

    log6 = math.log2(6.0)

    def up(log_in, log_out, to):
        return lambda i, rows: middle(i, 0, 0, up_in, up_out, to, log_in, log_out, rows)

    def down(log_in, log_out, to):
        return lambda i, rows: middle(i, 2, 1, dn_in, dn_out, to, log_in, log_out, rows)

    merged[:, lanes(TILES)] = jnp.zeros((8, LANES), F32)

    def whole(ref, sem):
        pltpu.make_async_copy(ref, ref, sem).wait()

    @pl.when(task == 0)
    def _():
        outer(0, 0, up_out, up_in, 1, 2, 1, dn_in)
        whole(up_out, chain_send.at[0])
        whole(seg_out, seg_send)

    @pl.when(task == 3)
    def _():
        outer(2, 1, dn_out, dn_in, 2, 0, 0, up_in)
        whole(dn_out, chain_send.at[1])
        whole(seg_out, seg_send)

    @pl.when(task == 1)
    def _():
        inner(up(1.0, 2.0, 2), down(2.0, log6, 0))
        whole(up_out, chain_send.at[0])
        whole(dn_out, chain_send.at[1])

    @pl.when(task == 2)
    def _():
        inner(down(1.0, 2.0, 1), up(2.0, log6, 3))
        whole(up_out, chain_send.at[0])
        whole(dn_out, chain_send.at[1])

    rest = split.at[:, pl.ds(0, 7)]
    whole(rest, out_send)
    whole(out, out_recv)


def body(adjusted, fisher):
    models, rows, columns = adjusted.shape
    shape = (models, ROWS, 8, columns)
    chain = pltpu.VMEM((ROWS, 2, 8, (1 + 2 * TILES) * LANES), BF16)
    out = pl.pallas_call(
        kernel,
        out_shape=jax.ShapeDtypeStruct((8, 8, ROWS, 8, LANES), BF16),
        in_specs=[pl.BlockSpec(memory_space=pl.ANY)] * 2,
        out_specs=pl.BlockSpec(memory_space=pltpu.VMEM),
        scratch_shapes=[
            pltpu.VMEM(shape, BF16),
            pltpu.VMEM(shape, BF16),
            chain, chain, chain, chain,
            pltpu.VMEM((8, (TILES + 1) * LANES), F32),
            pltpu.VMEM((ROWS, 2, 8, 8, SEG_PAD), BF16),
            pltpu.VMEM((ROWS, 8, 8, SEG_PAD), BF16),
            pltpu.VMEM((ROWS, 8, 8, 8, LANES), BF16),
            pltpu.SemaphoreType.DMA((2, ROWS)),
            pltpu.SemaphoreType.DMA((2, STEPS, len(PIECES))),
            pltpu.SemaphoreType.DMA((2,)),
            pltpu.SemaphoreType.DMA((ROWS,)),
            pltpu.SemaphoreType.DMA,
            pltpu.SemaphoreType.DMA,
            pltpu.SemaphoreType.DMA,
        ],
        compiler_params=pltpu.CompilerParams(collective_id=0, has_side_effects=True),
    )(adjusted.reshape(shape), fisher.reshape(shape))
    return out.reshape(-1, LANES)[:, :OWN]


def solution(mesh):
    return jax.shard_map(
        body,
        mesh=mesh,
        in_specs=(P("task", "tile", None), P("task", "tile", None)),
        out_specs=P(None, ("task", "tile")),
        check_vma=False,
    )
```

time: 302 us -> 97.6 us (0.32)
  waiting for transfers between devices: 181 us -> 0 us
  Pallas kernels: 0 us -> 95.1 us
  blocking collectives: 63.9 us -> 0 us
  local copies, waits for them, and re-layouts: 18.1 us -> 2.36 us
  between operations: 13.4 us -> 0.01 us
  starting transfers between devices: 12.1 us -> 0 us
  other arithmetic: 10.3 us -> 0 us
    reduce_scatter x1 -> x0, waiting for transfers between devices: 155 us -> none  [in_one_piece(): lax.psum_scatter(both, axis, scatter_dimension=dim, tiled=True)]
    pallas_call x0 -> x1, Pallas kernels: none -> 95.1 us  [body(): pl.pallas_call(kernel, out_shape=jax.ShapeDtypeStruct((8, 8, ROWS, 8, LAN...]
    all_to_all x1 -> x0, blocking collectives: 63.9 us -> none  [body(): lax.all_to_all(summed_num, 'tile', split_axis=1, concat_axis=0, tiled=True)]
    all_to_all x1 -> x0, waiting for transfers between devices: 26.1 us -> none  [body(): lax.all_to_all(summed_den, 'tile', split_axis=1, concat_axis=0, tiled=True)]
    all_to_all x4 -> x0, local copies, waits for them, and re-layouts: 14.2 us -> none  [the longest x2 7.92 us: body(): lax.all_to_all(summed_num, 'tile', split_axis=1, concat_axis=0, tiled=True)]
    all_to_all x1 -> x0, starting transfers between devices: 12.1 us -> none  [body(): lax.all_to_all(summed_den, 'tile', split_axis=1, concat_axis=0, tiled=True)]
    reduce_sum x1 -> x0, other arithmetic: 6.06 us -> none  [body(): numerator = jnp.sum(scaled * adjusted.astype(jnp.float32), axis=0)]
    concatenate x1 -> x0, other arithmetic: 3.84 us -> none  [in_one_piece(): both = jnp.concatenate(arrays, axis=along)]
  transfers between devices with their start and end apart: 2 -> 0, of which waited for: 2 -> 0; matrix products, arithmetic and copies ran while one was open for 1% -> 0% of each run, Pallas kernels for 0% -> 0%
where the time goes in v1:
time: 97.6 us; the launch traced here: 97.5 us
  Pallas kernels  95.1 us (97%)
  local copies, waits for them, and re-layouts  2.36 us (2%)
    pallas_call x1, Pallas kernels, body(): pl.pallas_call(kernel, out_shape=jax.ShapeDtypeStruct((8, 8, ROWS, 8, LAN...  95.1 us
    unnamed x1, local copies, waits for them, and re-layouts  2.36 us

profile of v1, /device:TPU:1, one launch (start us, length us, event | category | flops | bytes accessed | tf_op | source)
XLA Modules:
  0.0 97.5 jit_solution(8893181128481450462)
XLA Ops:
  0.0 95.1 %shard_map.28 = bf16[8,8,7,8,128]{4,3,2,1,0:T(8,128)(2,1)} custom-call(bf16[2,7,8,18944]{3,2,1,0:T(8,128)(2,1)} %bitcast.4, bf16[2,7,8,18944]{3,2,1,0:T(8,128)(2,1)} %bitcast.5), custom_call_target="tpu_custom_call" | custom-call | tf_op jit(solution)/shard_map/pallas_call | solution.py:331
  95.1 2.4 %copy.4 = bf16[3584,74]{0,1:T(8,128)(2,1)} copy(bf16[3584,74]{1,0:T(8,128)(2,1)} %bitcast.6) | data formatting | bytes 1060864

commit v2 on v1

--- a/solution.py
+++ b/solution.py
@@ -13,12 +13,15 @@
 BF16 = jnp.bfloat16
 
 ROWS, TILES, LANES = 7, 37, 128
-QUARTER = TILES * LANES
 SEG, SEG_PAD, OWN = 592, 640, 74
-PIECES = ((0, 19), (19, 18))
+PIECES = ((0, 10), (10, 9), (19, 9), (28, 9))
 GROUP = 5
 STEPS = 2 * ROWS
-AHEAD, LAG, SKEW = 5, 3, 2
+AHEAD, LAG, SKEW = 5, 3, 5
+EVEN = (*range(0, 5), *range(9, 14), *range(18, 23), *range(28, 32))
+ODD = (*range(5, 9), *range(14, 18), *range(23, 28), *range(32, 37))
+HEAD = {1: 48, 3: 16, 4: 0, 6: 32}
+TAIL = {1: 48, 3: 16, 4: 64, 6: 32}
 
 Q_POWER, Q_TOP, Q_KNEE = 24.0, 120.0, -9.5
 Q_FLOOR = 2.0 ** (Q_TOP + Q_POWER * Q_KNEE)
@@ -64,8 +67,8 @@
     return [range(a, min(a + GROUP, start + count)) for a in range(start, start + count, GROUP)]
 
 
-def kernel(a_hbm, f_hbm, out, av, fv, up_in, up_out, dn_in, dn_out, merged, seg_out, seg_in, split,
-           in_sem, chain_recv, chain_send, seg_recv, seg_send, out_recv, out_send):
+def kernel(a_hbm, f_hbm, out, av, fv, up_in, up_out, dn_in, dn_out, merged, seg_out, seg_in, edge_out, edge_in, split,
+           in_sem, chain_recv, chain_send, seg_recv, seg_send, edge_recv, edge_send, out_recv, out_send):
     task, tile = lax.axis_index("task"), lax.axis_index("tile")
     slot, side = tile // 8, tile % 8
 
@@ -77,6 +80,7 @@
         for copy in loads(r):
             copy.start()
 
+    edge_in[...] = jnp.zeros_like(edge_in)
     barrier = pltpu.get_barrier_semaphore()
     place = task * 8 + slot
 
@@ -91,7 +95,6 @@
 
     lax.fori_loop(1, 32, greet_column, 0)
     lax.fori_loop(1, 8, greet_side, 0)
-    pl.semaphore_wait(barrier, 38)
 
     def wait_rows(i):
         @pl.when(i % 2 == 0)
@@ -99,23 +102,32 @@
             for copy in loads(i // 2):
                 copy.wait()
 
-    def own(i, first_task, tiles):
-        r, t = i // 2, i % 2
-        base = (first_task + t) * TILES
+    half = slot % 2
+    odd_task = (3 * half, 3 - 3 * half)
+    even_task = (3 - 3 * half, 3 * half)
+
+    def column(i, way, x):
+        if x < len(ODD):
+            other = odd_task[way] * TILES + ODD[x]
+        else:
+            other = even_task[way] * TILES + EVEN[x - len(ODD)]
+        return lanes(jnp.where(i % 2 == 0, (1 + way) * TILES + x, other))
+
+    def own(i, way, tiles):
+        r = i // 2
         n, d = [], []
         for x in tiles:
-            at = lanes(base + x)
+            at = column(i, way, x)
             f0, f1 = fv[0, r, :, at].astype(F32), fv[1, r, :, at].astype(F32)
             n.append(f0 * av[0, r, :, at].astype(F32) + f1 * av[1, r, :, at].astype(F32))
             d.append(f0 + f1)
         return n, d
 
-    def own_scale(i, first_task):
-        r, t = i // 2, i % 2
-        base = (first_task + t) * TILES
+    def own_scale(i, way):
+        r = i // 2
         tops = [jnp.full((8, LANES), 2.0**-96, F32) for _ in range(4)]
         for x in range(TILES):
-            at = lanes(base + x)
+            at = column(i, way, x)
             for m in range(2):
                 k = (2 * x + m) % 4
                 tops[k] = jnp.maximum(tops[k], jnp.abs(av[m, r, :, at].astype(F32)))
@@ -156,74 +168,139 @@
         for x, code in zip(tiles, e):
             target[r, t, :, lanes(1 + start + count + x)] = code
 
-    def first(i, first_task, way, target, landing, to):
+    def first(i, way, target, landing, to, send=True):
         wait_rows(i)
-        scale = own_scale(i, first_task)
+        scale = own_scale(i, way)
         inverse = 1.0 / scale
         target[i // 2, i % 2, :, lanes(0)] = scale.astype(BF16)
         for piece, (start, count) in enumerate(PIECES):
             for tiles in groups(start, count):
-                n, d = own(i, first_task, tiles)
+                n, d = own(i, way, tiles)
                 put(i, piece, tiles, n, d, target, 1.0, inverse)
-            hop(i, piece, target, landing, way, to).start()
-
-    def middle(i, first_task, way, source, target, to, log_in, log_out, wait_for_rows):
-        if wait_for_rows:
-            wait_rows(i)
-        mine = own_scale(i, first_task)
-        for piece, (start, count) in enumerate(PIECES):
-            arrived(i, piece, source, way)
-            if piece == 0:
-                before = source[i // 2, i % 2, :, lanes(0)].astype(F32)
-                scale = jnp.maximum(before, mine)
-                inverse = 1.0 / scale
-                target[i // 2, i % 2, :, lanes(0)] = scale.astype(BF16)
-            for tiles in groups(start, count):
-                n, d = own(i, first_task, tiles)
-                q, e = received(i, piece, tiles, source, log_in, before)
-                n = [x + a * b for x, a, b in zip(n, q, e)]
-                d = [x + b for x, b in zip(d, e)]
-                put(i, piece, tiles, n, d, target, log_out, inverse)
-            hop(i, piece, target, source, way, to).start()
+            if send:
+                hop(i, piece, target, landing, way, to).start()
+
+    def middle(i, piece, way, source, target, to, log_in, log_out):
+        r, t = i // 2, i % 2
+        start, count = PIECES[piece]
+        if piece == 0:
+            mine = own_scale(i, way)
+        arrived(i, piece, source, way)
+        before = source[r, t, :, lanes(0)].astype(F32)
+        if piece == 0:
+            scale = jnp.maximum(before, mine)
+            target[r, t, :, lanes(0)] = scale.astype(BF16)
+        else:
+            scale = target[r, t, :, lanes(0)].astype(F32)
+        inverse = 1.0 / scale
+        for tiles in groups(start, count):
+            n, d = own(i, way, tiles)
+            q, e = received(i, piece, tiles, source, log_in, before)
+            n = [x + a * b for x, a, b in zip(n, q, e)]
+            d = [x + b for x, b in zip(d, e)]
+            put(i, piece, tiles, n, d, target, log_out, inverse)
+        hop(i, piece, target, source, way, to).start()
 
     lane = lax.broadcasted_iota(jnp.int32, (8, LANES), 1)
 
-    def last(i, first_task, way, source):
+    def last(i, way, source):
         r, t = i // 2, i % 2
         for piece, (start, count) in enumerate(PIECES):
             arrived(i, piece, source, way)
             if piece == 0:
                 before = source[r, t, :, lanes(0)].astype(F32)
             for tiles in groups(start, count):
-                n, d = own(i, first_task, tiles)
+                n, d = own(i, way, tiles)
                 q, e = received(i, piece, tiles, source, math.log2(6.0), before)
                 for x, n1, d1, q1, e1 in zip(tiles, n, d, q, e):
                     merged[:, lanes(x)] = (n1 + q1 * e1) / (d1 + e1)
-        for k in range(8):
-            low, off = SEG * k // LANES, SEG * k % LANES
-            parts = [merged[:, lanes(low + j)] for j in range(6 if off else 5)]
-            if off:
-                parts = [pltpu.roll(x, LANES - off, 1) for x in parts]
-                parts = [jnp.where(lane < LANES - off, parts[j], parts[j + 1]) for j in range(5)]
-            for j in range(5):
-                seg_out[r, t, k, :, lanes(j)] = parts[j].astype(BF16)
-        for k in range(8):
-            pltpu.make_async_remote_copy(
-                src_ref=seg_out.at[r, t, k], dst_ref=seg_in.at[r, slot],
-                send_sem=seg_send, recv_sem=seg_recv.at[r],
-                device_id=(first_task + t, k * 8 + side), device_id_type=MESH).start()
+
+        def shift(where, k):
+            part = merged[:, lanes(where)]
+            return pltpu.roll(part, LANES - SEG * k % LANES, 1) if SEG * k % LANES else part
+
+        def join(low, high, edge):
+            if low is None or high is None:
+                return high if low is None else low
+            return jnp.where(lane < edge, low, high)
+
+        def pack(place_of):
+            for k in range(8):
+                low, off = SEG * k // LANES, SEG * k % LANES
+                held = [place_of(k, low + j) for j in range(6 if off else 5)]
+                parts = [None if x is None else shift(x, k) for x in held]
+                for j in range(5):
+                    part = join(parts[j], parts[j + 1], LANES - off) if off else parts[j]
+                    seg_out[r, 8 * t + k, :, lanes(j)] = part.astype(BF16)
+
+        @pl.when(t == 0)
+        def _():
+            pack(lambda k, x: x if x < TILES else None)
+            for k in range(8):
+                pltpu.make_async_remote_copy(
+                    src_ref=seg_out.at[r, k], dst_ref=seg_in.at[r, slot],
+                    send_sem=seg_send, recv_sem=seg_recv.at[r],
+                    device_id=(1 + way, k * 8 + side), device_id_type=MESH).start()
+
+        @pl.when(t == 1)
+        def _():
+            def place_of(k, x):
+                if k % 2:
+                    return ODD.index(x) if x in ODD else None
+                return len(ODD) + EVEN.index(x) if x in EVEN else None
+
+            pack(place_of)
+            for e, k in enumerate(sorted(HEAD)):
+                first_tile, last_tile = SEG * k // LANES, (SEG * (k + 1) - 1) // LANES
+                low = None if HEAD[k] == 0 else shift(place_of(k + 1, first_tile), k)
+                edge_out[r, e] = join(low, shift(place_of(k + 1, last_tile), k), HEAD[k]).astype(BF16)
+            for k in range(8):
+                to = odd_task[way] if k % 2 else even_task[way]
+                mine = (to == task) & (k == slot)
+
+                @pl.when(mine)
+                def _():
+                    pltpu.make_async_copy(seg_out.at[r, 8 + k], seg_in.at[r, slot], seg_recv.at[r]).start()
+
+                @pl.when(jnp.logical_not(mine))
+                def _():
+                    pltpu.make_async_remote_copy(
+                        src_ref=seg_out.at[r, 8 + k], dst_ref=seg_in.at[r, slot],
+                        send_sem=seg_send, recv_sem=seg_recv.at[r],
+                        device_id=(to, k * 8 + side), device_id_type=MESH).start()
+            for e, k in enumerate(sorted(HEAD)):
+                to = even_task[way] if k % 2 else odd_task[way]
+                pltpu.make_async_remote_copy(
+                    src_ref=edge_out.at[r, e], dst_ref=edge_in.at[r, slot],
+                    send_sem=edge_send, recv_sem=edge_recv.at[r],
+                    device_id=(to, k * 8 + side), device_id_type=MESH).start()
 
     lane3 = lax.broadcasted_iota(jnp.int32, (8, 8, LANES), 2)
+
+    shared = (task % 3 == 0) & ((slot % 5 == 1) | (slot == 3) | (slot == 4))
+    head, tail = jnp.int32(0), jnp.int32(LANES)
+    for k in HEAD:
+        head = jnp.where(shared & (slot == k), HEAD[k], head)
+        tail = jnp.where(shared & (slot == k), TAIL[k], tail)
 
     def spread(r):
         pltpu.make_async_copy(seg_in.at[r], seg_in.at[r], seg_recv.at[r]).wait()
+
+        @pl.when(shared)
+        def _():
+            pltpu.make_async_copy(edge_in.at[r], edge_in.at[r], edge_recv.at[r]).wait()
+
+        edge = edge_in[r].astype(F32)
+        tiles = [seg_in[r, :, :, lanes(j)].astype(F32) for j in range(5)]
+        tiles[0] = jnp.where(lane3 < head, edge, tiles[0])
+        tiles[4] = jnp.where(lane3 >= tail, edge, tiles[4])
         for k in range(8):
             low, off = OWN * k // LANES, OWN * k % LANES
-            part = seg_in[r, :, :, lanes(low)].astype(F32)
+            part = tiles[low]
             if off:
                 part = pltpu.roll(part, LANES - off, 2)
             if off + OWN > LANES:
-                more = pltpu.roll(seg_in[r, :, :, lanes(low + 1)].astype(F32), LANES - off, 2)
+                more = pltpu.roll(tiles[low + 1], LANES - off, 2)
                 part = jnp.where(lane3 < LANES - off, part, more)
             split[r, k] = part.astype(BF16)
         pltpu.make_async_copy(split.at[r, side], out.at[:, side, r], out_recv).start()
@@ -245,14 +322,16 @@
 
         lax.fori_loop(low, high, step, 0)
 
-    def outer(send_task, send_way, target, landing, to, merge_task, merge_way, source):
+    def outer(send_way, target, landing, to, merge_way, source):
         def go(i):
-            first(i, send_task, send_way, target, landing, to)
-
-        loop(0, AHEAD, go)
+            first(i, send_way, target, landing, to)
+
+        for piece in range(len(PIECES)):
+            hop(0, piece, target, landing, send_way, to).start()
+        loop(1, AHEAD, go)
 
         def step(i):
-            last(i, merge_task, merge_way, source)
+            last(i, merge_way, source)
 
             @pl.when(i + AHEAD < STEPS)
             def _():
@@ -269,43 +348,61 @@
         def step(i):
             @pl.when(i < STEPS)
             def _():
-                lead(i, True)
-
-            @pl.when(i >= SKEW)
-            def _():
-                trail(i - SKEW, False)
-
-            @pl.when((i % 2 == 1) & (i // 2 >= LAG))
+                wait_rows(i)
+
+            for piece in range(len(PIECES)):
+                back, late = (piece - SKEW) // len(PIECES), (piece - SKEW) % len(PIECES)
+
+                @pl.when(i < STEPS)
+                def _():
+                    lead(i, piece)
+
+                @pl.when((i + back >= 0) & (i + back < STEPS))
+                def _():
+                    trail(i + back, late)
+
+            @pl.when((i % 2 == 1) & (i // 2 >= LAG) & (i // 2 - LAG < ROWS))
             def _():
                 spread(i // 2 - LAG)
 
-        loop(0, STEPS + SKEW, step)
-        loop((STEPS + SKEW) // 2 - LAG, ROWS, spread)
+        steps = STEPS - (-SKEW // len(PIECES))
+        loop(0, steps, step)
+        loop(max(steps // 2 - LAG, 0), ROWS, spread)
 
     log6 = math.log2(6.0)
 
     def up(log_in, log_out, to):
-        return lambda i, rows: middle(i, 0, 0, up_in, up_out, to, log_in, log_out, rows)
+        return lambda i, piece: middle(i, piece, 0, up_in, up_out, to, log_in, log_out)
 
     def down(log_in, log_out, to):
-        return lambda i, rows: middle(i, 2, 1, dn_in, dn_out, to, log_in, log_out, rows)
-
-    merged[:, lanes(TILES)] = jnp.zeros((8, LANES), F32)
+        return lambda i, piece: middle(i, piece, 1, dn_in, dn_out, to, log_in, log_out)
+
+    @pl.when(task == 0)
+    def _():
+        first(0, 0, up_out, up_in, 1, False)
+
+    @pl.when(task == 3)
+    def _():
+        first(0, 1, dn_out, dn_in, 2, False)
+
+    pl.semaphore_wait(barrier, 38)
 
     def whole(ref, sem):
         pltpu.make_async_copy(ref, ref, sem).wait()
 
     @pl.when(task == 0)
     def _():
-        outer(0, 0, up_out, up_in, 1, 2, 1, dn_in)
+        outer(0, up_out, up_in, 1, 1, dn_in)
         whole(up_out, chain_send.at[0])
-        whole(seg_out, seg_send)
+        whole(seg_out.at[:, pl.ds(0, 15)], seg_send)
+        whole(edge_out, edge_send)
 
     @pl.when(task == 3)
     def _():
-        outer(2, 1, dn_out, dn_in, 2, 0, 0, up_in)
+        outer(1, dn_out, dn_in, 2, 0, up_in)
         whole(dn_out, chain_send.at[1])
-        whole(seg_out, seg_send)
+        whole(seg_out.at[:, pl.ds(0, 15)], seg_send)
+        whole(edge_out, edge_send)
 
     @pl.when(task == 1)
     def _():
@@ -337,13 +434,17 @@
             pltpu.VMEM(shape, BF16),
             pltpu.VMEM(shape, BF16),
             chain, chain, chain, chain,
-            pltpu.VMEM((8, (TILES + 1) * LANES), F32),
-            pltpu.VMEM((ROWS, 2, 8, 8, SEG_PAD), BF16),
+            pltpu.VMEM((8, TILES * LANES), F32),
+            pltpu.VMEM((ROWS, 16, 8, SEG_PAD), BF16),
             pltpu.VMEM((ROWS, 8, 8, SEG_PAD), BF16),
+            pltpu.VMEM((ROWS, len(HEAD), 8, LANES), BF16),
+            pltpu.VMEM((ROWS, 8, 8, LANES), BF16),
             pltpu.VMEM((ROWS, 8, 8, 8, LANES), BF16),
             pltpu.SemaphoreType.DMA((2, ROWS)),
             pltpu.SemaphoreType.DMA((2, STEPS, len(PIECES))),
             pltpu.SemaphoreType.DMA((2,)),
+            pltpu.SemaphoreType.DMA((ROWS,)),
+            pltpu.SemaphoreType.DMA,
             pltpu.SemaphoreType.DMA((ROWS,)),
             pltpu.SemaphoreType.DMA,
             pltpu.SemaphoreType.DMA,

time: 97.6 us -> 89.5 us (0.917)
  Pallas kernels: 95.1 us -> 87 us
    pallas_call x1, Pallas kernels: 95.1 us -> 87 us  [body(): pl.pallas_call(kernel, out_shape=jax.ShapeDtypeStruct((8, 8, ROWS, 8, LAN...]
where the time goes in v2:
time: 89.5 us; the launch traced here: 89.4 us
  Pallas kernels  87 us (97%)
  local copies, waits for them, and re-layouts  2.36 us (3%)
    pallas_call x1, Pallas kernels, body(): pl.pallas_call(kernel, out_shape=jax.ShapeDtypeStruct((8, 8, ROWS, 8, LAN...  87 us
    unnamed x1, local copies, waits for them, and re-layouts  2.36 us

profile of v2, /device:TPU:1, one launch (start us, length us, event | category | flops | bytes accessed | tf_op | source)
XLA Modules:
  0.0 89.4 jit_solution(605181944754901903)
XLA Ops:
  0.0 87.0 %shard_map.28 = bf16[8,8,7,8,128]{4,3,2,1,0:T(8,128)(2,1)} custom-call(bf16[2,7,8,18944]{3,2,1,0:T(8,128)(2,1)} %bitcast.4, bf16[2,7,8,18944]{3,2,1,0:T(8,128)(2,1)} %bitcast.5), custom_call_target="tpu_custom_call" | custom-call | tf_op jit(solution)/shard_map/pallas_call | solution.py:428
  87.0 2.4 %copy.4 = bf16[3584,74]{0,1:T(8,128)(2,1)} copy(bf16[3584,74]{1,0:T(8,128)(2,1)} %bitcast.6) | data formatting | bytes 1060864

commit v3 on v2

--- a/solution.py
+++ b/solution.py
@@ -17,7 +17,8 @@
 PIECES = ((0, 10), (10, 9), (19, 9), (28, 9))
 GROUP = 5
 STEPS = 2 * ROWS
-AHEAD, LAG, SKEW = 5, 3, 5
+AHEAD, LAG, DELAY, SKEW = 5, 2, 7, 5
+HELD, RELEASE, HOLD_OTHER = 5, 9, True
 EVEN = (*range(0, 5), *range(9, 14), *range(18, 23), *range(28, 32))
 ODD = (*range(5, 9), *range(14, 18), *range(23, 28), *range(32, 37))
 HEAD = {1: 48, 3: 16, 4: 0, 6: 32}
@@ -203,6 +204,17 @@
 
     lane = lax.broadcasted_iota(jnp.int32, (8, LANES), 1)
 
+    def hand_in(r, way, z):
+        def send(y, carry):
+            k = 2 * y + z
+            pltpu.make_async_remote_copy(
+                src_ref=seg_out.at[r, k], dst_ref=seg_in.at[r, half, slot // 2],
+                send_sem=seg_send, recv_sem=seg_recv.at[r, half],
+                device_id=(1 + way, k * 8 + side), device_id_type=MESH).start()
+            return carry
+
+        lax.fori_loop(0, 4, send, 0)
+
     def last(i, way, source):
         r, t = i // 2, i % 2
         for piece, (start, count) in enumerate(PIECES):
@@ -236,11 +248,14 @@
         @pl.when(t == 0)
         def _():
             pack(lambda k, x: x if x < TILES else None)
-            for k in range(8):
-                pltpu.make_async_remote_copy(
-                    src_ref=seg_out.at[r, k], dst_ref=seg_in.at[r, slot],
-                    send_sem=seg_send, recv_sem=seg_recv.at[r],
-                    device_id=(1 + way, k * 8 + side), device_id_type=MESH).start()
+            if not HOLD_OTHER:
+                hand_in(r, way, 1 - half)
+
+            @pl.when(r >= HELD)
+            def _():
+                hand_in(r, way, half)
+                if HOLD_OTHER:
+                    hand_in(r, way, 1 - half)
 
         @pl.when(t == 1)
         def _():
@@ -260,22 +275,23 @@
 
                 @pl.when(mine)
                 def _():
-                    pltpu.make_async_copy(seg_out.at[r, 8 + k], seg_in.at[r, slot], seg_recv.at[r]).start()
+                    pltpu.make_async_copy(
+                        seg_out.at[r, 8 + k], seg_in.at[r, half, slot // 2], seg_recv.at[r, half]).start()
 
                 @pl.when(jnp.logical_not(mine))
                 def _():
                     pltpu.make_async_remote_copy(
-                        src_ref=seg_out.at[r, 8 + k], dst_ref=seg_in.at[r, slot],
-                        send_sem=seg_send, recv_sem=seg_recv.at[r],
+                        src_ref=seg_out.at[r, 8 + k], dst_ref=seg_in.at[r, half, slot // 2],
+                        send_sem=seg_send, recv_sem=seg_recv.at[r, half],
                         device_id=(to, k * 8 + side), device_id_type=MESH).start()
             for e, k in enumerate(sorted(HEAD)):
                 to = even_task[way] if k % 2 else odd_task[way]
                 pltpu.make_async_remote_copy(
-                    src_ref=edge_out.at[r, e], dst_ref=edge_in.at[r, slot],
-                    send_sem=edge_send, recv_sem=edge_recv.at[r],
+                    src_ref=edge_out.at[r, e], dst_ref=edge_in.at[r, half, slot // 2],
+                    send_sem=edge_send, recv_sem=edge_recv.at[r, half],
                     device_id=(to, k * 8 + side), device_id_type=MESH).start()
 
-    lane3 = lax.broadcasted_iota(jnp.int32, (8, 8, LANES), 2)
+    lane3 = lax.broadcasted_iota(jnp.int32, (4, 8, LANES), 2)
 
     shared = (task % 3 == 0) & ((slot % 5 == 1) | (slot == 3) | (slot == 4))
     head, tail = jnp.int32(0), jnp.int32(LANES)
@@ -283,15 +299,15 @@
         head = jnp.where(shared & (slot == k), HEAD[k], head)
         tail = jnp.where(shared & (slot == k), TAIL[k], tail)
 
-    def spread(r):
-        pltpu.make_async_copy(seg_in.at[r], seg_in.at[r], seg_recv.at[r]).wait()
+    def spread(r, z):
+        pltpu.make_async_copy(seg_in.at[r, z], seg_in.at[r, z], seg_recv.at[r, z]).wait()
 
         @pl.when(shared)
         def _():
-            pltpu.make_async_copy(edge_in.at[r], edge_in.at[r], edge_recv.at[r]).wait()
-
-        edge = edge_in[r].astype(F32)
-        tiles = [seg_in[r, :, :, lanes(j)].astype(F32) for j in range(5)]
+            pltpu.make_async_copy(edge_in.at[r, z], edge_in.at[r, z], edge_recv.at[r, z]).wait()
+
+        edge = edge_in[r, z].astype(F32)
+        tiles = [seg_in[r, z, :, :, lanes(j)].astype(F32) for j in range(5)]
         tiles[0] = jnp.where(lane3 < head, edge, tiles[0])
         tiles[4] = jnp.where(lane3 >= tail, edge, tiles[4])
         for k in range(8):
@@ -302,13 +318,13 @@
             if off + OWN > LANES:
                 more = pltpu.roll(tiles[low + 1], LANES - off, 2)
                 part = jnp.where(lane3 < LANES - off, part, more)
-            split[r, k] = part.astype(BF16)
-        pltpu.make_async_copy(split.at[r, side], out.at[:, side, r], out_recv).start()
+            split[r, z, k] = part.astype(BF16)
+        pltpu.make_async_copy(split.at[r, z, side], out.at[:, z, side, r], out_recv).start()
 
         def send(i, carry):
             k = (side + i) % 8
             pltpu.make_async_remote_copy(
-                src_ref=split.at[r, k], dst_ref=out.at[:, side, r],
+                src_ref=split.at[r, z, k], dst_ref=out.at[:, z, side, r],
                 send_sem=out_send, recv_sem=out_recv,
                 device_id=(task, slot * 8 + k), device_id_type=MESH).start()
             return carry
@@ -332,6 +348,14 @@
 
         def step(i):
             last(i, merge_way, source)
+            for j in range(2):
+                held = i - RELEASE + j
+
+                @pl.when((held % 2 == j) & (held >= j) & (held < HELD))
+                def _():
+                    hand_in(held, merge_way, half)
+                    if HOLD_OTHER:
+                        hand_in(held, merge_way, 1 - half)
 
             @pl.when(i + AHEAD < STEPS)
             def _():
@@ -339,10 +363,10 @@
 
             @pl.when((i % 2 == 1) & (i // 2 >= LAG))
             def _():
-                spread(i // 2 - LAG)
+                loop(0, 2, lambda z: spread(i // 2 - LAG, z))
 
         loop(0, STEPS, step)
-        loop(ROWS - LAG, ROWS, spread)
+        loop(2 * (ROWS - LAG), 2 * ROWS, lambda i: spread(i // 2, i % 2))
 
     def inner(lead, trail):
         def step(i):
@@ -361,13 +385,22 @@
                 def _():
                     trail(i + back, late)
 
-            @pl.when((i % 2 == 1) & (i // 2 >= LAG) & (i // 2 - LAG < ROWS))
-            def _():
-                spread(i // 2 - LAG)
+            @pl.when((i % 2 == 1) & (i // 2 >= DELAY))
+            def _():
+                spread(i // 2 - DELAY, 1 - half)
 
         steps = STEPS - (-SKEW // len(PIECES))
         loop(0, steps, step)
-        loop(max(steps // 2 - LAG, 0), ROWS, spread)
+        done = steps // 2 - DELAY
+
+        def finish(r):
+            spread(r, half)
+
+            @pl.when(r >= done)
+            def _():
+                spread(r, 1 - half)
+
+        loop(0, ROWS, finish)
 
     log6 = math.log2(6.0)
 
@@ -416,7 +449,7 @@
         whole(up_out, chain_send.at[0])
         whole(dn_out, chain_send.at[1])
 
-    rest = split.at[:, pl.ds(0, 7)]
+    rest = split.at[:, :, pl.ds(0, 7)]
     whole(rest, out_send)
     whole(out, out_recv)
 
@@ -427,25 +460,25 @@
     chain = pltpu.VMEM((ROWS, 2, 8, (1 + 2 * TILES) * LANES), BF16)
     out = pl.pallas_call(
         kernel,
-        out_shape=jax.ShapeDtypeStruct((8, 8, ROWS, 8, LANES), BF16),
+        out_shape=jax.ShapeDtypeStruct((4, 2, 8, ROWS, 8, LANES), BF16),
         in_specs=[pl.BlockSpec(memory_space=pl.ANY)] * 2,
-        out_specs=pl.BlockSpec(memory_space=pltpu.VMEM),
+        out_specs=pl.BlockSpec(memory_space=pl.ANY),
         scratch_shapes=[
             pltpu.VMEM(shape, BF16),
             pltpu.VMEM(shape, BF16),
             chain, chain, chain, chain,
             pltpu.VMEM((8, TILES * LANES), F32),
             pltpu.VMEM((ROWS, 16, 8, SEG_PAD), BF16),
-            pltpu.VMEM((ROWS, 8, 8, SEG_PAD), BF16),
+            pltpu.VMEM((ROWS, 2, 4, 8, SEG_PAD), BF16),
             pltpu.VMEM((ROWS, len(HEAD), 8, LANES), BF16),
-            pltpu.VMEM((ROWS, 8, 8, LANES), BF16),
-            pltpu.VMEM((ROWS, 8, 8, 8, LANES), BF16),
+            pltpu.VMEM((ROWS, 2, 4, 8, LANES), BF16),
+            pltpu.VMEM((ROWS, 2, 8, 4, 8, LANES), BF16),
             pltpu.SemaphoreType.DMA((2, ROWS)),
             pltpu.SemaphoreType.DMA((2, STEPS, len(PIECES))),
             pltpu.SemaphoreType.DMA((2,)),
-            pltpu.SemaphoreType.DMA((ROWS,)),
+            pltpu.SemaphoreType.DMA((ROWS, 2)),
             pltpu.SemaphoreType.DMA,
-            pltpu.SemaphoreType.DMA((ROWS,)),
+            pltpu.SemaphoreType.DMA((ROWS, 2)),
             pltpu.SemaphoreType.DMA,
             pltpu.SemaphoreType.DMA,
             pltpu.SemaphoreType.DMA,

time: 89.5 us -> 84 us (0.939)
  Pallas kernels: 87 us -> 81.5 us
    pallas_call x1, Pallas kernels: 87 us -> 81.5 us  [body(): pl.pallas_call(kernel, out_shape=jax.ShapeDtypeStruct((4, 2, 8, ROWS, 8,...]
where the time goes in v3:
time: 84 us; the launch traced here: 83.9 us
  Pallas kernels  81.5 us (97%)
  local copies, waits for them, and re-layouts  2.36 us (3%)
    pallas_call x1, Pallas kernels, body(): pl.pallas_call(kernel, out_shape=jax.ShapeDtypeStruct((4, 2, 8, ROWS, 8,...  81.5 us
    unnamed x1, local copies, waits for them, and re-layouts  2.36 us

profile of v3, /device:TPU:1, one launch (start us, length us, event | category | flops | bytes accessed | tf_op | source)
XLA Modules:
  0.0 83.9 jit_solution(17317838316047194886)
XLA Ops:
  0.0 81.5 %shard_map.28 = bf16[4,2,8,7,8,128]{5,4,3,2,1,0:T(8,128)(2,1)} custom-call(bf16[2,7,8,18944]{3,2,1,0:T(8,128)(2,1)} %bitcast.4, bf16[2,7,8,18944]{3,2,1,0:T(8,128)(2,1)} %bitcast.5), custom_call_target="tpu_custom_call" | custom-call | tf_op jit(solution)/shard_map/pallas_call | solution.py:461
  81.5 2.4 %copy.4 = bf16[3584,74]{0,1:T(8,128)(2,1)} copy(bf16[3584,74]{1,0:T(8,128)(2,1)} %bitcast.6) | data formatting | bytes 1060864

commit v4 on v3

--- a/solution.py
+++ b/solution.py
@@ -17,7 +17,7 @@
 PIECES = ((0, 10), (10, 9), (19, 9), (28, 9))
 GROUP = 5
 STEPS = 2 * ROWS
-AHEAD, LAG, DELAY, SKEW = 5, 2, 7, 5
+AHEAD, LAG, DELAY, SKEW = 5, 1, 7, 5
 HELD, RELEASE, HOLD_OTHER = 5, 9, True
 EVEN = (*range(0, 5), *range(9, 14), *range(18, 23), *range(28, 32))
 ODD = (*range(5, 9), *range(14, 18), *range(23, 28), *range(32, 37))

time: 84 us -> 84.2 us (level)
  no operation moved by 1% of the time
where the time goes in v4:
time: 84.2 us; the launch traced here: 83.9 us
  Pallas kernels  81.5 us (97%)
  local copies, waits for them, and re-layouts  2.36 us (3%)
    pallas_call x1, Pallas kernels, body(): pl.pallas_call(kernel, out_shape=jax.ShapeDtypeStruct((4, 2, 8, ROWS, 8,...  81.5 us
    unnamed x1, local copies, waits for them, and re-layouts  2.36 us

profile of v4, /device:TPU:1, one launch (start us, length us, event | category | flops | bytes accessed | tf_op | source)
XLA Modules:
  0.0 83.9 jit_solution(9463699016710417519)
XLA Ops:
  0.0 81.5 %shard_map.28 = bf16[4,2,8,7,8,128]{5,4,3,2,1,0:T(8,128)(2,1)} custom-call(bf16[2,7,8,18944]{3,2,1,0:T(8,128)(2,1)} %bitcast.4, bf16[2,7,8,18944]{3,2,1,0:T(8,128)(2,1)} %bitcast.5), custom_call_target="tpu_custom_call" | custom-call | tf_op jit(solution)/shard_map/pallas_call | solution.py:461
  81.5 2.4 %copy.4 = bf16[3584,74]{0,1:T(8,128)(2,1)} copy(bf16[3584,74]{1,0:T(8,128)(2,1)} %bitcast.6) | data formatting | bytes 1060864
